TPU v7x, 512 devices: a 4x2x32 block of a 4x8x32 slice. The times are simulated.
512 devices in a mesh: parts: 2 (over y), expert: 64 (over z, core), tensor: 4 (over x).
Axes of the slice: x: 4, y: 2, z: 32, core: 2. Of those that a mesh axis runs over, the one named last changes fastest.
The devices are a block of a 4x8x32 slice.
Arguments:
- tokens: bfloat16 [2048, 6144], P(('parts', 'expert'), 'tensor'), parts along dimension 0, may hold values from -4 to 4
- queries: bfloat16 [2048, 48, 128], P(('parts', 'expert'), 'tensor'), parts along dimension 0, may hold values from -6 to 6
- new_kv: bfloat16 [2, 2048, 8, 128], P(None, ('parts', 'expert'), 'tensor'), parts along dimension 1, may hold values from -6 to 6
- cache_kv: bfloat16 [2, 2048, 16, 8, 128], P(None, ('parts', 'expert'), None, 'tensor'), parts along dimension 1, may hold values from -6 to 6
- lengths: int32 [2048], P(('parts', 'expert')), parts along dimension 0, may hold values from 2 to 16
- gain: float32 [6144], P('tensor'), may hold values from 0.1 to 1.9
- gate_weight: bfloat16 [6144, 32768], P('tensor', 'expert'), may hold values from -0.078125 to 0.078125
- up_weight: bfloat16 [6144, 32768], P('tensor', 'expert'), may hold values from -0.078125 to 0.078125
- down_weight: bfloat16 [32768, 6144], P('expert', 'tensor'), may hold values from -0.0625 to 0.0625
- routes: int32 [2048, 2], P(('parts', 'expert')), parts along dimension 0, may hold values from 0 to 3, all different within a row; in each aligned block of 16 rows (0 to 15, 16 to 31, ...) at most 9 rows name the same one
- route_weights: bfloat16 [2048, 2], P(('parts', 'expert')), parts along dimension 0, may hold values from 0.19921875 to 0.796875
Outputs:
- mixed: bfloat16 [2048, 6144], P(('parts', 'expert'), 'tensor'), parts along dimension 0
There are 2 independent parts, one for each index of `parts`. A program takes and returns all parts, laid end to end along the dimension named above; an argument that names none is the same for every part. Nothing has to cross between parts.
Inputs may be any that keep to these rules, and one draw needn't show every extreme that they name: `routes`: the two entries of a row differ; in the rows of one index of expert no expert is named more than 9 times, a bound that some block reaches there in every draw.
All inputs are finite; a program needn't handle non-finite values.
Results may differ from a plain program's by a relative error of at most 0.0094.
Values may be sent and summed in bfloat16 or wider, within the bound.
No kernel may reach another device: no remote copies, remote signals or barrier semaphores. Data moves between devices by JAX's collectives and lax.ppermute only.
A program may use at most 64 MiB of HBM per device.

v0:
```python
import functools
import math

import jax
import jax.numpy as jnp
from jax import lax
from jax.experimental import pallas as pl
from jax.experimental.pallas import tpu as pltpu
from jax.sharding import Mesh
from jax.sharding import PartitionSpec as P


EXPERTS = 4
CAP = 9
EXPERT = ("seg", "pos", "core")
PARTS_EXPERT = ("parts", "seg", "pos", "core")
LANES = 128

EPSILON = 1e-05


def from_partner(x, axis, apart):
    return lax.ppermute(x, axis, [(i, i ^ apart) for i in range(lax.axis_size(axis))])


def pack_kernel(*refs):
    sources, (residual_ref, packed_ref, mixing_ref) = refs[:8], refs[8:11]
    rows_ref, here, arrived = refs[11], refs[12:20], refs[20]
    copies = [
        pltpu.make_async_copy(source, target, arrived.at[i])
        for i, (source, target) in enumerate(zip(sources, here))
    ]
    for copy in copies:
        copy.start()
    for copy in copies:
        copy.wait()
    cache_ref, queries_ref, new_ref, tokens_ref, gain_ref, lengths_ref, routes_ref, weights_ref = here
    count, head_size = queries_ref.shape
    sequences, _ = tokens_ref.shape
    heads = count // sequences
    key_heads = new_ref.shape[1] // sequences
    cached = cache_ref.shape[1]
    places = cached // (sequences * key_heads)
    group = heads // key_heads
    factor = 1.0 / math.sqrt(head_size)

    def matching(shape, per_sequence):
        row = lax.broadcasted_iota(jnp.int32, shape, 0)
        column = lax.broadcasted_iota(jnp.int32, shape, 1)
        same = row % sequences == column // per_sequence
        return same & (row // (sequences * group) == column % key_heads)

    queries = queries_ref[...]
    across = (((1,), (1,)), ((), ()))
    old = lax.dot_general(queries, cache_ref[0], across, preferred_element_type=jnp.float32) * factor
    new = lax.dot_general(queries, new_ref[0], across, preferred_element_type=jnp.float32) * factor
    limit = jnp.zeros((1, cached), jnp.int32)
    column = lax.broadcasted_iota(jnp.int32, (1, cached), 1)
    for i in range(sequences):
        limit = jnp.where(column // (places * key_heads) == i, lengths_ref[i], limit)
    usable = column // key_heads % places < limit
    old = jnp.where(matching(old.shape, places * key_heads) & usable, old, -jnp.inf)
    new = jnp.where(matching(new.shape, key_heads), new, -jnp.inf)
    largest = jnp.maximum(jnp.max(old, axis=1, keepdims=True), jnp.max(new, axis=1, keepdims=True))
    old = jnp.exp(old - largest)
    new = jnp.exp(new - largest)
    total = jnp.sum(old, axis=1, keepdims=True) + jnp.sum(new, axis=1, keepdims=True)
    old = (old / total).astype(jnp.bfloat16)
    new = (new / total).astype(jnp.bfloat16)
    rows_ref[...] = jnp.dot(old, cache_ref[1], preferred_element_type=jnp.float32) + jnp.dot(
        new, new_ref[1], preferred_element_type=jnp.float32
    )
    slots = packed_ref.shape[0]
    slot = lax.broadcasted_iota(jnp.int32, (slots, sequences), 0)
    column = lax.broadcasted_iota(jnp.int32, (1, sequences), 1)
    targets = [jnp.zeros((1, sequences), jnp.int32) for _ in range(2)]
    used = [jnp.int32(0)] * EXPERTS
    for i in range(sequences):
        for j in range(2):
            route = routes_ref[j, i]
            target = jnp.int32(0)
            for k in range(EXPERTS):
                target = jnp.where(route == k, k * CAP + used[k], target)
                used[k] = used[k] + jnp.where(route == k, 1, 0)
            targets[j] = jnp.where(column == i, target, targets[j])
    weights = weights_ref[...].astype(jnp.float32)
    mixing = jnp.where(slot == targets[0], weights[0:1], 0.0)
    mixing_ref[...] = jnp.where(slot == targets[1], weights[1:2], mixing).astype(jnp.bfloat16)
    placing = jnp.where((slot == targets[0]) | (slot == targets[1]), 1.0, 0.0).astype(jnp.bfloat16)
    for h in range(heads):
        at = slice(h * head_size, (h + 1) * head_size)
        attended = rows_ref[h * sequences : (h + 1) * sequences, :]
        residual = tokens_ref[:, at].astype(jnp.float32) + attended
        residual_ref[:, at] = residual
        scaled = (residual * gain_ref[h : h + 1]).astype(jnp.bfloat16)
        packed = jnp.dot(placing, scaled, preferred_element_type=jnp.float32)
        packed_ref[:, at] = packed.astype(jnp.bfloat16)


def pack_part(tokens, queries, new_kv, cache_kv, lengths, gain, routes, route_weights):
    sequences, width = tokens.shape
    _, heads, head_size = queries.shape
    slots = EXPERTS * CAP
    whole = pl.BlockSpec(memory_space=pltpu.VMEM)
    arrays = (
        cache_kv.reshape(2, -1, head_size),
        queries.transpose(1, 0, 2).reshape(heads * sequences, head_size),
        new_kv.reshape(2, -1, head_size),
        tokens,
        gain.reshape(heads, head_size),
        lengths,
        routes.T,
        route_weights.T,
    )
    places = [pltpu.SMEM if a.dtype == jnp.int32 else pltpu.VMEM for a in arrays]
    return pl.pallas_call(
        pack_kernel,
        out_shape=[
            pltpu.VMEM((sequences, width), jnp.float32),
            pltpu.VMEM((slots, width), jnp.bfloat16),
            pltpu.VMEM((slots, sequences), jnp.bfloat16),
        ],
        in_specs=[pl.BlockSpec(memory_space=pltpu.HBM)] * len(arrays),
        out_specs=[whole] * 3,
        scratch_shapes=[
            pltpu.VMEM((sequences * heads, head_size), jnp.float32),
            *(place(a.shape, a.dtype) for place, a in zip(places, arrays)),
            pltpu.SemaphoreType.DMA((len(arrays),)),
        ],
        compiler_params=pltpu.CompilerParams(vmem_limit_bytes=16 << 20),
        name="pack",
    )(*(pltpu.with_memory_space_constraint(a, pltpu.HBM) for a in arrays))


def between_segments(blocks):
    segs, places, cores = (lax.axis_size(a) for a in EXPERT)
    groups = [
        [
            (seg * places + (place + places // 2 * (2 * seg // segs)) % places) * cores + core
            for seg in range(segs)
        ]
        for place in range(places)
        for core in range(cores)
    ]
    return lax.all_to_all(
        blocks, EXPERT, split_axis=0, concat_axis=0, tiled=True, axis_index_groups=groups
    )


def kept(x):
    return pltpu.with_memory_space_constraint(x, pltpu.VMEM)


def up_kernel(*refs):
    pieces, (gain_ref, gate_ref, up_ref, out_ref, rows_ref) = refs[:-5], refs[-5:]
    across, share, _ = out_ref.shape
    columns = gate_ref.shape[1]
    count = pieces[0].shape[0]
    inverse = 1.0 / gain_ref[...]
    lane = lax.broadcasted_iota(jnp.int32, (count, LANES), 1)
    for i, piece in enumerate(pieces):
        rows = piece[...]
        rows_ref[i * count : (i + 1) * count, :] = rows
        squares = jnp.zeros((count, LANES), jnp.float32)
        for c in range(inverse.shape[0]):
            plain = rows[:, c * LANES : (c + 1) * LANES].astype(jnp.float32) * inverse[c : c + 1]
            squares = squares + plain * plain
        squares = jnp.sum(squares, axis=1, keepdims=True)
        high = squares.astype(jnp.bfloat16).astype(jnp.float32)
        both = jnp.where(lane == 0, high, squares - high).astype(jnp.bfloat16)
        out_ref[i, :, 2 * columns :] = both
    for at, weight in ((0, gate_ref), (columns, up_ref)):
        sums = jnp.dot(rows_ref[...], weight[...], preferred_element_type=jnp.float32)
        sums = sums.astype(jnp.bfloat16)
        for i in range(across):
            out_ref[i, :, at : at + columns] = sums[i * share : (i + 1) * share]


def up_part(pieces, gain, gate_weight, up_weight):
    count, local_width = pieces[0].shape
    columns = gate_weight.shape[1]
    across = lax.axis_size("tensor")
    assert across == len(pieces)
    whole = pl.BlockSpec(memory_space=pltpu.VMEM)
    return pl.pallas_call(
        up_kernel,
        out_shape=pltpu.VMEM((across, count, 2 * columns + LANES), jnp.bfloat16),
        in_specs=[whole] * (len(pieces) + 3),
        out_specs=whole,
        scratch_shapes=[pltpu.VMEM((len(pieces) * count, local_width), jnp.bfloat16)],
        compiler_params=pltpu.CompilerParams(vmem_limit_bytes=16 << 20),
        name="up",
    )(*map(kept, (*pieces, gain.reshape(-1, LANES), gate_weight, up_weight)))


def hidden_kernel(full_width, sums_ref, out_ref):
    across, _, width = sums_ref.shape
    columns = (width - LANES) // 2
    total = sums_ref[0].astype(jnp.float32)
    for i in range(1, across):
        total = total + sums_ref[i].astype(jnp.float32)
    squares = total[:, 2 * columns : 2 * columns + 1] + total[:, 2 * columns + 1 : 2 * columns + 2]
    scale = lax.rsqrt(squares / full_width + EPSILON)
    gate = total[:, :columns] * scale
    lift = total[:, columns : 2 * columns] * scale
    hidden = (gate / (1.0 + jnp.exp(-gate)) * lift).astype(jnp.bfloat16)
    for i in range(across):
        out_ref[i] = hidden


def activated(sums, full_width):
    across, count, width = sums.shape
    whole = pl.BlockSpec(memory_space=pltpu.VMEM)
    return pl.pallas_call(
        functools.partial(hidden_kernel, full_width),
        out_shape=pltpu.VMEM((across, count, (width - LANES) // 2), jnp.bfloat16),
        in_specs=[whole],
        out_specs=whole,
        compiler_params=pltpu.CompilerParams(vmem_limit_bytes=8 << 20),
        name="hidden",
    )(kept(sums))


def send(x):
    return x.astype(jnp.bfloat16)


def gathered(own):
    by4 = from_partner(own, "pos", 4)
    by2 = from_partner(own, "pos", 2)
    by6 = from_partner(by4, "pos", 2)
    near = jnp.concatenate([own, by4], axis=0)
    far = jnp.concatenate([by2, by6], axis=0)
    near_next = from_partner(near, "pos", 1)
    far_next = from_partner(far, "pos", 1)
    held = jnp.concatenate([near, far], axis=0)
    held_there = from_partner(held, "core", 1)
    following = jnp.concatenate([near_next, far_next], axis=0)
    following_there = from_partner(following, "core", 1)
    return held, following, held_there, following_there


def down_kernel(hidden_ref, weight_ref, *outs):
    count = hidden_ref.shape[1]
    hidden = hidden_ref[...].reshape(-1, hidden_ref.shape[2])
    width = weight_ref.shape[1] // 3
    for start in range(0, 3 * width, width):
        columns = slice(start, start + width)
        terms = jnp.dot(hidden, weight_ref[:, columns], preferred_element_type=jnp.float32)
        for i, out in enumerate(outs):
            out[:, columns] = terms[i * count : (i + 1) * count].astype(out.dtype)


def down_part(hidden, down_weight):
    _, count, _ = hidden.shape
    width = down_weight.shape[1]
    whole = pl.BlockSpec(memory_space=pltpu.VMEM)
    kinds = (jnp.float32, jnp.float32, jnp.bfloat16, jnp.bfloat16)
    return pl.pallas_call(
        down_kernel,
        out_shape=[pltpu.VMEM((count, width), kind) for kind in kinds],
        in_specs=[whole, whole],
        out_specs=[whole] * len(kinds),
        compiler_params=pltpu.CompilerParams(vmem_limit_bytes=16 << 20),
        name="down",
    )(kept(hidden), kept(down_weight))


def summed(held, following, held_there, following_there):
    half = held.shape[0] // 2
    own = half // 2
    here = from_partner(following_there, "core", 1).astype(jnp.float32)
    following = send(following + here)
    held = held + from_partner(held_there, "core", 1).astype(jnp.float32)
    near, far = lax.optimization_barrier((held[:half], held[half:]))
    far = far + from_partner(following[half:], "pos", 1).astype(jnp.float32)
    near = near + from_partner(following[:half], "pos", 1).astype(jnp.float32)
    far = send(far)
    by4 = near[own:] + from_partner(far[own:], "pos", 2).astype(jnp.float32)
    home = near[:own] + from_partner(far[:own], "pos", 2).astype(jnp.float32)
    return home + from_partner(send(by4), "pos", 4).astype(jnp.float32)


def through_expert(pieces, gain, gate_weight, up_weight, down_weight):
    across = lax.axis_size("tensor")
    sums = up_part(pieces, gain, gate_weight, up_weight)
    sums = lax.all_to_all(sums, "tensor", split_axis=0, concat_axis=0, tiled=True)
    copies = activated(sums, gate_weight.shape[0] * across)
    hidden = lax.all_to_all(copies, "tensor", split_axis=0, concat_axis=0, tiled=True)
    return down_part(hidden, down_weight)


def on_device(
    tokens,
    queries,
    new_kv,
    cache_kv,
    lengths,
    gain,
    gate_weight,
    up_weight,
    down_weight,
    routes,
    route_weights,
):
    _, local_width = tokens.shape
    residual, packed, mixing = pack_part(
        tokens, queries, new_kv, cache_kv, lengths, gain, routes, route_weights
    )
    flat = packed.reshape(EXPERTS, CAP * local_width // LANES, LANES)
    rows = between_segments(flat).reshape(EXPERTS * CAP, local_width)
    terms = through_expert(gathered(rows), gain, gate_weight, up_weight, down_weight)
    results = summed(*terms).astype(jnp.bfloat16)
    per_slot = between_segments(results.reshape(flat.shape)).reshape(EXPERTS * CAP, local_width)
    moe_sum = lax.dot_general(
        mixing, per_slot, (((0,), (0,)), ((), ())), preferred_element_type=jnp.float32
    )
    return (residual + moe_sum).astype(jnp.bfloat16)


def solution(mesh):
    split = Mesh(
        mesh.devices.reshape(
            mesh.shape["parts"], EXPERTS, mesh.shape["expert"] // (2 * EXPERTS), 2, mesh.shape["tensor"]
        ),
        ("parts", "seg", "pos", "core", "tensor"),
    )
    return jax.shard_map(
        on_device,
        mesh=split,
        in_specs=(
            P(PARTS_EXPERT, "tensor"),
            P(PARTS_EXPERT, "tensor", None),
            P(None, PARTS_EXPERT, "tensor", None),
            P(None, PARTS_EXPERT, None, "tensor", None),
            P(PARTS_EXPERT),
            P("tensor"),
            P("tensor", EXPERT),
            P("tensor", EXPERT),
            P(EXPERT, "tensor"),
            P(PARTS_EXPERT, None),
            P(PARTS_EXPERT, None),
        ),
        out_specs=P(PARTS_EXPERT, "tensor"),
        check_vma=False,
    )
```

profile of v0, /device:TPU:40, one launch (start us, length us, event | category | flops | bytes accessed | tf_op | source)
XLA Modules:
  0.0 210.4 jit_solution(17810154121285606385)
XLA Ops:
  0.0 1.9 pack.1
  1.9 0.2 reshape.29
  2.0 0.0 copy-start.1
  2.0 0.0 copy-start.2
  2.0 0.0 copy-start.3
  2.1 61.9 %all_to_all.20 = bf16[4,108,128]{2,1,0:T(8,128)(2,1)S(1)} all-to-all(bf16[4,108,128]{2,1,0:T(8,128)(2,1)S(1)} %reshape.29), channel_id=1, replica_groups={{0,64,160,224},{4,68,164,228},{8,72,168,232},{12,76,172,236},{16,80,176..., dimensions={0} | all-to-all | bytes 221184 | tf_op jit(solution)/shard_map/all_to_all | solution.py:145
  64.0 0.2 reshape.30
  64.1 13.4 %collective-permute-start = (bf16[36,1536]{1,0:T(8,128)(2,1)S(1)}, bf16[36,1536]{1,0:T(8,128)(2,1)S(1)}, u32[]{:S(2)}, u32[]{:S(2)}) collective-permute-start(bf16[36,1536]{1,0:T(8,128)(2,1)S(1)} %reshape.30), channel_id=1, source_target_pairs={{0,32},{8,40},{16,48},{24,56},{32,0},{40,8},{48,16},{56,24},{1,33}... | collective-permute-start | bytes 331784 | tf_op jit(solution)/shard_map/ppermute | solution.py:23
  77.5 2.3 %collective-permute-start.1 = (bf16[36,1536]{1,0:T(8,128)(2,1)S(1)}, bf16[36,1536]{1,0:T(8,128)(2,1)S(1)}, u32[]{:S(2)}, u32[]{:S(2)}) collective-permute-start(bf16[36,1536]{1,0:T(8,128)(2,1)S(1)} %reshape.30), channel_id=1, source_target_pairs={{0,16},{8,24},{16,0},{24,8},{32,48},{40,56},{48,32},{56,40},{1,17}... | collective-permute-start | bytes 331784 | tf_op jit(solution)/shard_map/ppermute | solution.py:23
  79.8 5.3 %collective-permute-done = bf16[36,1536]{1,0:T(8,128)(2,1)S(1)} collective-permute-done((bf16[36,1536]{1,0:T(8,128)(2,1)S(1)}, bf16[36,1536]{1,0:T(8,128)(2,1)S(1)}, u32[]{:S(2)}, u32[]{:S(2)}) %collective-permute-start) | collective-permute-done | bytes 110624 | tf_op jit(solution)/shard_map/ppermute | solution.py:23
  85.1 4.2 %collective-permute-start.2 = (bf16[36,1536]{1,0:T(8,128)(2,1)S(1)}, bf16[36,1536]{1,0:T(8,128)(2,1)S(1)}, u32[]{:S(2)}, u32[]{:S(2)}) collective-permute-start(bf16[36,1536]{1,0:T(8,128)(2,1)S(1)} %collective-permute-done), channel_id=1, source_target_pairs={{0,16},{8,24},{16,0},{24,8},{32,48},{40,56},{48,32},{56,40},{1,17}... | collective-permute-start | bytes 331784 | tf_op jit(solution)/shard_map/ppermute | solution.py:23
  89.4 2.7 %collective-permute-start.3 = (bf16[72,1536]{1,0:T(8,128)(2,1)S(1)}, bf16[72,1536]{1,0:T(8,128)(2,1)S(1)}, u32[]{:S(2)}, u32[]{:S(2)}) collective-permute-start(bf16[72,1536]{1,0:T(8,128)(2,1)S(1)} %pad_maximum_fusion.1), channel_id=1, source_target_pairs={{0,8},{8,0},{16,24},{24,16},{32,40},{40,32},{48,56},{56,48},{1,9},... | collective-permute-start | bytes 663560 | tf_op jit(solution)/shard_map/ppermute | solution.py:23
  92.1 0.0 collective-permute-done.1
  92.1 2.3 %collective-permute-done.2 = bf16[36,1536]{1,0:T(8,128)(2,1)S(1)} collective-permute-done((bf16[36,1536]{1,0:T(8,128)(2,1)S(1)}, bf16[36,1536]{1,0:T(8,128)(2,1)S(1)}, u32[]{:S(2)}, u32[]{:S(2)}) %collective-permute-start.2) | collective-permute-done | bytes 110624 | tf_op jit(solution)/shard_map/ppermute | solution.py:23
  94.5 2.4 %collective-permute-start.4 = (bf16[72,1536]{1,0:T(8,128)(2,1)S(1)}, bf16[72,1536]{1,0:T(8,128)(2,1)S(1)}, u32[]{:S(2)}, u32[]{:S(2)}) collective-permute-start(bf16[72,1536]{1,0:T(8,128)(2,1)S(1)} %pad_maximum_fusion.2), channel_id=1, source_target_pairs={{0,8},{8,0},{16,24},{24,16},{32,40},{40,32},{48,56},{56,48},{1,9},... | collective-permute-start | bytes 663560 | tf_op jit(solution)/shard_map/ppermute | solution.py:23
  96.9 0.1 pad_maximum_fusion.refs_0_
  97.0 2.0 collective-permute-start.5
  99.0 0.6 collective-permute-done.3
  99.6 3.7 %collective-permute-done.4 = bf16[72,1536]{1,0:T(8,128)(2,1)S(1)} collective-permute-done((bf16[72,1536]{1,0:T(8,128)(2,1)S(1)}, bf16[72,1536]{1,0:T(8,128)(2,1)S(1)}, u32[]{:S(2)}, u32[]{:S(2)}) %collective-permute-start.4) | collective-permute-done | bytes 221216 | tf_op jit(solution)/shard_map/ppermute | solution.py:23
  103.4 2.0 collective-permute-start.6
  105.3 0.0 collective-permute-done.5.refs_2_
  105.4 1.7 collective-permute-done.6.refs_3_
  107.1 0.0 copy-done.1
  107.1 0.0 copy-done.2
  107.1 0.0 copy-done.3
  107.1 2.2 %up.1 = bf16[4,144,1152]{2,1,0:T(8,128)(2,1)S(1)} custom-call(bf16[144,1536]{1,0:T(8,128)(2,1)S(1)} %pad_maximum_fusion.refs_0_, bf16[144,1536]{1,0:T(8,128)(2,1)S(1)} %constant_dynamic-update-slice_fusion.refs_1_, bf16[144,1536]{1,0:T(8,128)(2,1)S(1)} %collective-permute-done.5.refs_2_, bf16[144,1536]{1,0:T(8,128)(2,1)S(1)} %collective-permute-done.6.refs_3_, ...), custom_call_target="tpu_custom_call" | custom-call | tf_op jit(solution)/shard_map/up/pallas_call | solution.py:185
  109.3 22.8 %all_to_all.21.sums_ref = bf16[4,144,1152]{2,1,0:T(8,128)(2,1)S(1)} all-to-all(bf16[4,144,1152]{2,1,0:T(8,128)(2,1)S(1)} %up.1), channel_id=1, replica_groups=mesh['parts'=2,'seg'=4,'pos'=8,'core'=2,'tensor'=4] {'tensor'}, dimensions={0} | all-to-all | bytes 2654208 | tf_op jit(solution)/shard_map/all_to_all | solution.py:287
  132.1 0.0 copy-start
  132.1 0.3 hidden.1
  132.4 12.2 %all_to_all.22.hidden_ref = bf16[4,144,512]{2,1,0:T(8,128)(2,1)S(1)} all-to-all(bf16[4,144,512]{2,1,0:T(8,128)(2,1)S(1)} %hidden.1), channel_id=1, replica_groups=mesh['parts'=2,'seg'=4,'pos'=8,'core'=2,'tensor'=4] {'tensor'}, dimensions={0} | all-to-all | bytes 1179648 | tf_op jit(solution)/shard_map/all_to_all | solution.py:289
  144.6 0.0 copy-done
  144.6 1.1 down.1
  145.7 2.0 collective-permute-start.8
  147.6 2.4 %collective-permute-start.7 = (bf16[144,1536]{1,0:T(8,128)(2,1)S(1)}, bf16[144,1536]{1,0:T(8,128)(2,1)S(1)}, u32[]{:S(2)}, u32[]{:S(2)}) collective-permute-start(bf16[144,1536]{1,0:T(8,128)(2,1)S(1)} %get-tuple-element.18), channel_id=1, source_target_pairs={{0,4},{4,0},{1,5},{5,1},{2,6},{6,2},{3,7},{7,3},{8,12},{12,8},{9,1... | collective-permute-start | bytes 1327112 | tf_op jit(solution)/shard_map/ppermute | solution.py:23
  150.1 0.0 collective-permute-done.8
  150.1 0.1 add_convert_fusion
  150.2 2.7 %collective-permute-start.10 = (bf16[72,1536]{1,0:T(8,128)(2,1)S(1)}, bf16[72,1536]{1,0:T(8,128)(2,1)S(1)}, u32[]{:S(2)}, u32[]{:S(2)}) collective-permute-start(bf16[72,1536]{1,0:T(8,128)(2,1)S(1)} %get-tuple-element.25), channel_id=1, source_target_pairs={{0,8},{8,0},{16,24},{24,16},{32,40},{40,32},{48,56},{56,48},{1,9},... | collective-permute-start | bytes 663560 | tf_op jit(solution)/shard_map/ppermute | solution.py:23
  152.9 0.0 collective-permute-done.7
  152.9 0.1 convert_add_fusion
  153.0 0.1 fusion.4
  153.0 3.2 %collective-permute-start.9 = (bf16[72,1536]{1,0:T(8,128)(2,1)S(1)}, bf16[72,1536]{1,0:T(8,128)(2,1)S(1)}, u32[]{:S(2)}, u32[]{:S(2)}) collective-permute-start(bf16[72,1536]{1,0:T(8,128)(2,1)S(1)} %get-tuple-element.26), channel_id=1, source_target_pairs={{0,8},{8,0},{16,24},{24,16},{32,40},{40,32},{48,56},{56,48},{1,9},... | collective-permute-start | bytes 663560 | tf_op jit(solution)/shard_map/ppermute | solution.py:23
  156.3 4.1 %collective-permute-done.10 = bf16[72,1536]{1,0:T(8,128)(2,1)S(1)} collective-permute-done((bf16[72,1536]{1,0:T(8,128)(2,1)S(1)}, bf16[72,1536]{1,0:T(8,128)(2,1)S(1)}, u32[]{:S(2)}, u32[]{:S(2)}) %collective-permute-start.10) | collective-permute-done | bytes 221216 | tf_op jit(solution)/shard_map/ppermute | solution.py:23
  160.5 4.3 %collective-permute-start.12 = (bf16[36,1536]{1,0:T(8,128)(2,1)S(1)}, bf16[36,1536]{1,0:T(8,128)(2,1)S(1)}, u32[]{:S(2)}, u32[]{:S(2)}) collective-permute-start(bf16[36,1536]{1,0:T(8,128)(2,1)S(1)} %get-tuple-element.28), channel_id=1, source_target_pairs={{0,16},{8,24},{16,0},{24,8},{32,48},{40,56},{48,32},{56,40},{1,17}... | collective-permute-start | bytes 331784 | tf_op jit(solution)/shard_map/ppermute | solution.py:23
  164.8 2.5 %collective-permute-start.11 = (bf16[36,1536]{1,0:T(8,128)(2,1)S(1)}, bf16[36,1536]{1,0:T(8,128)(2,1)S(1)}, u32[]{:S(2)}, u32[]{:S(2)}) collective-permute-start(bf16[36,1536]{1,0:T(8,128)(2,1)S(1)} %get-tuple-element.27), channel_id=1, source_target_pairs={{0,16},{8,24},{16,0},{24,8},{32,48},{40,56},{48,32},{56,40},{1,17}... | collective-permute-start | bytes 331784 | tf_op jit(solution)/shard_map/ppermute | solution.py:23
  167.3 0.0 collective-permute-done.9
  167.3 0.1 convert_add_fusion.1
  167.4 4.9 %collective-permute-done.12 = bf16[36,1536]{1,0:T(8,128)(2,1)S(1)} collective-permute-done((bf16[36,1536]{1,0:T(8,128)(2,1)S(1)}, bf16[36,1536]{1,0:T(8,128)(2,1)S(1)}, u32[]{:S(2)}, u32[]{:S(2)}) %collective-permute-start.12) | collective-permute-done | bytes 110624 | tf_op jit(solution)/shard_map/ppermute | solution.py:23
  172.4 6.0 %collective-permute-start.13 = (bf16[36,1536]{1,0:T(8,128)(2,1)S(1)}, bf16[36,1536]{1,0:T(8,128)(2,1)S(1)}, u32[]{:S(2)}, u32[]{:S(2)}) collective-permute-start(bf16[36,1536]{1,0:T(8,128)(2,1)S(1)} %fusion.1), channel_id=1, source_target_pairs={{0,32},{8,40},{16,48},{24,56},{32,0},{40,8},{48,16},{56,24},{1,33}... | collective-permute-start | bytes 331784 | tf_op jit(solution)/shard_map/ppermute | solution.py:23
  178.4 0.0 collective-permute-done.11
  178.4 10.3 %collective-permute-done.13 = bf16[36,1536]{1,0:T(8,128)(2,1)S(1)} collective-permute-done((bf16[36,1536]{1,0:T(8,128)(2,1)S(1)}, bf16[36,1536]{1,0:T(8,128)(2,1)S(1)}, u32[]{:S(2)}, u32[]{:S(2)}) %collective-permute-start.13) | collective-permute-done | bytes 110624 | tf_op jit(solution)/shard_map/ppermute | solution.py:23
  188.7 0.2 reshape.31
  188.9 20.5 %all_to_all.23 = bf16[4,108,128]{2,1,0:T(8,128)(2,1)S(1)} all-to-all(bf16[4,108,128]{2,1,0:T(8,128)(2,1)S(1)} %reshape.31), channel_id=1, replica_groups={{0,64,160,224},{4,68,164,228},{8,72,168,232},{12,76,172,236},{16,80,176..., dimensions={0} | all-to-all | bytes 221184 | tf_op jit(solution)/shard_map/all_to_all | solution.py:145
  209.4 0.2 reshape.32
  209.5 0.8 fusion
  (9 shorter events, 0.3 us)
Async XLA Ops:
  2.0 105.1 %copy-start.1 = (bf16[1536,512]{1,0:T(8,128)(2,1)S(1)}, bf16[1536,512]{1,0:T(8,128)(2,1)}, u32[]{:S(2)}) copy-start(bf16[1536,512]{1,0:T(8,128)(2,1)} %refs_5_.3) | copy-start | bytes 4718596
  2.0 105.1 %copy-start.2 = (bf16[1536,512]{1,0:T(8,128)(2,1)S(1)}, bf16[1536,512]{1,0:T(8,128)(2,1)}, u32[]{:S(2)}) copy-start(bf16[1536,512]{1,0:T(8,128)(2,1)} %refs_6_.1) | copy-start | bytes 4718596
  2.0 105.1 %copy-start.3 = (f32[1536]{0:T(1024)S(1)}, f32[1536]{0:T(1024)}, u32[]{:S(2)}) copy-start(f32[1536]{0:T(1024)} %param.16) | copy-start | bytes 18436
  64.1 21.0 %collective-permute-start = (bf16[36,1536]{1,0:T(8,128)(2,1)S(1)}, bf16[36,1536]{1,0:T(8,128)(2,1)S(1)}, u32[]{:S(2)}, u32[]{:S(2)}) collective-permute-start(bf16[36,1536]{1,0:T(8,128)(2,1)S(1)} %reshape.30), channel_id=1, source_target_pairs={{0,32},{8,40},{16,48},{24,56},{32,0},{40,8},{48,16},{56,24},{1,33}... | collective-permute-start | bytes 331784 | tf_op jit(solution)/shard_map/ppermute | solution.py:23
  77.5 14.6 %collective-permute-start.1 = (bf16[36,1536]{1,0:T(8,128)(2,1)S(1)}, bf16[36,1536]{1,0:T(8,128)(2,1)S(1)}, u32[]{:S(2)}, u32[]{:S(2)}) collective-permute-start(bf16[36,1536]{1,0:T(8,128)(2,1)S(1)} %reshape.30), channel_id=1, source_target_pairs={{0,16},{8,24},{16,0},{24,8},{32,48},{40,56},{48,32},{56,40},{1,17}... | collective-permute-start | bytes 331784 | tf_op jit(solution)/shard_map/ppermute | solution.py:23
  85.1 9.4 %collective-permute-start.2 = (bf16[36,1536]{1,0:T(8,128)(2,1)S(1)}, bf16[36,1536]{1,0:T(8,128)(2,1)S(1)}, u32[]{:S(2)}, u32[]{:S(2)}) collective-permute-start(bf16[36,1536]{1,0:T(8,128)(2,1)S(1)} %collective-permute-done), channel_id=1, source_target_pairs={{0,16},{8,24},{16,0},{24,8},{32,48},{40,56},{48,32},{56,40},{1,17}... | collective-permute-start | bytes 331784 | tf_op jit(solution)/shard_map/ppermute | solution.py:23
  89.4 10.2 %collective-permute-start.3 = (bf16[72,1536]{1,0:T(8,128)(2,1)S(1)}, bf16[72,1536]{1,0:T(8,128)(2,1)S(1)}, u32[]{:S(2)}, u32[]{:S(2)}) collective-permute-start(bf16[72,1536]{1,0:T(8,128)(2,1)S(1)} %pad_maximum_fusion.1), channel_id=1, source_target_pairs={{0,8},{8,0},{16,24},{24,16},{32,40},{40,32},{48,56},{56,48},{1,9},... | collective-permute-start | bytes 663560 | tf_op jit(solution)/shard_map/ppermute | solution.py:23
  94.5 8.8 %collective-permute-start.4 = (bf16[72,1536]{1,0:T(8,128)(2,1)S(1)}, bf16[72,1536]{1,0:T(8,128)(2,1)S(1)}, u32[]{:S(2)}, u32[]{:S(2)}) collective-permute-start(bf16[72,1536]{1,0:T(8,128)(2,1)S(1)} %pad_maximum_fusion.2), channel_id=1, source_target_pairs={{0,8},{8,0},{16,24},{24,16},{32,40},{40,32},{48,56},{56,48},{1,9},... | collective-permute-start | bytes 663560 | tf_op jit(solution)/shard_map/ppermute | solution.py:23
  97.0 8.3 %collective-permute-start.5 = (bf16[144,1536]{1,0:T(8,128)(2,1)S(1)}, bf16[144,1536]{1,0:T(8,128)(2,1)S(1)}, u32[]{:S(2)}, u32[]{:S(2)}) collective-permute-start(bf16[144,1536]{1,0:T(8,128)(2,1)S(1)} %pad_maximum_fusion.refs_0_), channel_id=1, source_target_pairs={{0,4},{4,0},{1,5},{5,1},{2,6},{6,2},{3,7},{7,3},{8,12},{12,8},{9,1... | collective-permute-start | bytes 1327112 | tf_op jit(solution)/shard_map/ppermute | solution.py:23
  103.4 3.7 %collective-permute-start.6 = (bf16[144,1536]{1,0:T(8,128)(2,1)S(1)}, bf16[144,1536]{1,0:T(8,128)(2,1)S(1)}, u32[]{:S(2)}, u32[]{:S(2)}) collective-permute-start(bf16[144,1536]{1,0:T(8,128)(2,1)S(1)} %constant_dynamic-update-slice_fusion.refs_1_), channel_id=1, source_target_pairs={{0,4},{4,0},{1,5},{5,1},{2,6},{6,2},{3,7},{7,3},{8,12},{12,8},{9,1... | collective-permute-start | bytes 1327112 | tf_op jit(solution)/shard_map/ppermute | solution.py:23
  132.1 12.5 %copy-start = (bf16[512,1536]{1,0:T(8,128)(2,1)S(1)}, bf16[512,1536]{1,0:T(8,128)(2,1)}, u32[]{:S(2)}) copy-start(bf16[512,1536]{1,0:T(8,128)(2,1)} %weight_ref.1) | copy-start | bytes 4718596
  145.7 4.4 %collective-permute-start.8 = (bf16[144,1536]{1,0:T(8,128)(2,1)S(1)}, bf16[144,1536]{1,0:T(8,128)(2,1)S(1)}, u32[]{:S(2)}, u32[]{:S(2)}) collective-permute-start(bf16[144,1536]{1,0:T(8,128)(2,1)S(1)} %get-tuple-element.21), channel_id=1, source_target_pairs={{0,4},{4,0},{1,5},{5,1},{2,6},{6,2},{3,7},{7,3},{8,12},{12,8},{9,1... | collective-permute-start | bytes 1327112 | tf_op jit(solution)/shard_map/ppermute | solution.py:23
  147.6 5.3 %collective-permute-start.7 = (bf16[144,1536]{1,0:T(8,128)(2,1)S(1)}, bf16[144,1536]{1,0:T(8,128)(2,1)S(1)}, u32[]{:S(2)}, u32[]{:S(2)}) collective-permute-start(bf16[144,1536]{1,0:T(8,128)(2,1)S(1)} %get-tuple-element.18), channel_id=1, source_target_pairs={{0,4},{4,0},{1,5},{5,1},{2,6},{6,2},{3,7},{7,3},{8,12},{12,8},{9,1... | collective-permute-start | bytes 1327112 | tf_op jit(solution)/shard_map/ppermute | solution.py:23
  150.2 10.2 %collective-permute-start.10 = (bf16[72,1536]{1,0:T(8,128)(2,1)S(1)}, bf16[72,1536]{1,0:T(8,128)(2,1)S(1)}, u32[]{:S(2)}, u32[]{:S(2)}) collective-permute-start(bf16[72,1536]{1,0:T(8,128)(2,1)S(1)} %get-tuple-element.25), channel_id=1, source_target_pairs={{0,8},{8,0},{16,24},{24,16},{32,40},{40,32},{48,56},{56,48},{1,9},... | collective-permute-start | bytes 663560 | tf_op jit(solution)/shard_map/ppermute | solution.py:23
  153.0 14.3 %collective-permute-start.9 = (bf16[72,1536]{1,0:T(8,128)(2,1)S(1)}, bf16[72,1536]{1,0:T(8,128)(2,1)S(1)}, u32[]{:S(2)}, u32[]{:S(2)}) collective-permute-start(bf16[72,1536]{1,0:T(8,128)(2,1)S(1)} %get-tuple-element.26), channel_id=1, source_target_pairs={{0,8},{8,0},{16,24},{24,16},{32,40},{40,32},{48,56},{56,48},{1,9},... | collective-permute-start | bytes 663560 | tf_op jit(solution)/shard_map/ppermute | solution.py:23
  160.5 11.8 %collective-permute-start.12 = (bf16[36,1536]{1,0:T(8,128)(2,1)S(1)}, bf16[36,1536]{1,0:T(8,128)(2,1)S(1)}, u32[]{:S(2)}, u32[]{:S(2)}) collective-permute-start(bf16[36,1536]{1,0:T(8,128)(2,1)S(1)} %get-tuple-element.28), channel_id=1, source_target_pairs={{0,16},{8,24},{16,0},{24,8},{32,48},{40,56},{48,32},{56,40},{1,17}... | collective-permute-start | bytes 331784 | tf_op jit(solution)/shard_map/ppermute | solution.py:23
  164.8 13.5 %collective-permute-start.11 = (bf16[36,1536]{1,0:T(8,128)(2,1)S(1)}, bf16[36,1536]{1,0:T(8,128)(2,1)S(1)}, u32[]{:S(2)}, u32[]{:S(2)}) collective-permute-start(bf16[36,1536]{1,0:T(8,128)(2,1)S(1)} %get-tuple-element.27), channel_id=1, source_target_pairs={{0,16},{8,24},{16,0},{24,8},{32,48},{40,56},{48,32},{56,40},{1,17}... | collective-permute-start | bytes 331784 | tf_op jit(solution)/shard_map/ppermute | solution.py:23
  172.4 16.3 %collective-permute-start.13 = (bf16[36,1536]{1,0:T(8,128)(2,1)S(1)}, bf16[36,1536]{1,0:T(8,128)(2,1)S(1)}, u32[]{:S(2)}, u32[]{:S(2)}) collective-permute-start(bf16[36,1536]{1,0:T(8,128)(2,1)S(1)} %fusion.1), channel_id=1, source_target_pairs={{0,32},{8,40},{16,48},{24,56},{32,0},{40,8},{48,16},{56,24},{1,33}... | collective-permute-start | bytes 331784 | tf_op jit(solution)/shard_map/ppermute | solution.py:23
where the time goes:
time: 211 us; the launch traced here: 210 us
  blocking collectives  117 us (55%)
  starting transfers between devices  52 us (25%)
  waiting for transfers between devices  33.1 us (16%)
  Pallas kernels  5.45 us (3%)
    all_to_all x2, blocking collectives, between_segments(): lax.all_to_all(blocks, EXPERT, split_axis=0, concat_axis=0, tiled=True, a...  82.4 us
    ppermute x14, starting transfers between devices, from_partner(): lax.ppermute(x, axis, [(i, i ^ apart) for i in range(lax.axis_size(axis))])  52 us
    ppermute x14, waiting for transfers between devices, from_partner(): lax.ppermute(x, axis, [(i, i ^ apart) for i in range(lax.axis_size(axis))])  33.1 us
    all_to_all x1, blocking collectives, through_expert(): lax.all_to_all(sums, 'tensor', split_axis=0, concat_axis=0, tiled=True)  22.8 us
    all_to_all x1, blocking collectives, through_expert(): lax.all_to_all(copies, 'tensor', split_axis=0, concat_axis=0, tiled=True)  12.2 us
  transfers between devices with their start and end apart: 14, of which 8 were waited for; matrix products, arithmetic and copies ran while one was open for 0% of the time, Pallas kernels for 0%

commit v1 on v0

--- a/solution.py
+++ b/solution.py
@@ -153,7 +153,7 @@
 
 def up_kernel(*refs):
     pieces, (gain_ref, gate_ref, up_ref, out_ref, rows_ref) = refs[:-5], refs[-5:]
-    across, share, _ = out_ref.shape
+    across, share = out_ref.shape[0], out_ref.shape[1] // 2
     columns = gate_ref.shape[1]
     count = pieces[0].shape[0]
     inverse = 1.0 / gain_ref[...]
@@ -168,12 +168,13 @@
         squares = jnp.sum(squares, axis=1, keepdims=True)
         high = squares.astype(jnp.bfloat16).astype(jnp.float32)
         both = jnp.where(lane == 0, high, squares - high).astype(jnp.bfloat16)
-        out_ref[i, :, 2 * columns :] = both
-    for at, weight in ((0, gate_ref), (columns, up_ref)):
+        out_ref[i, :share, columns:] = both
+        out_ref[i, share:, columns:] = jnp.zeros_like(both)
+    for at, weight in ((0, gate_ref), (share, up_ref)):
         sums = jnp.dot(rows_ref[...], weight[...], preferred_element_type=jnp.float32)
         sums = sums.astype(jnp.bfloat16)
         for i in range(across):
-            out_ref[i, :, at : at + columns] = sums[i * share : (i + 1) * share]
+            out_ref[i, at : at + share, :columns] = sums[i * share : (i + 1) * share]
 
 
 def up_part(pieces, gain, gate_weight, up_weight):
@@ -184,7 +185,7 @@
     whole = pl.BlockSpec(memory_space=pltpu.VMEM)
     return pl.pallas_call(
         up_kernel,
-        out_shape=pltpu.VMEM((across, count, 2 * columns + LANES), jnp.bfloat16),
+        out_shape=pltpu.VMEM((across, 2 * count, columns + LANES), jnp.bfloat16),
         in_specs=[whole] * (len(pieces) + 3),
         out_specs=whole,
         scratch_shapes=[pltpu.VMEM((len(pieces) * count, local_width), jnp.bfloat16)],
@@ -194,15 +195,14 @@
 
 
 def hidden_kernel(full_width, sums_ref, out_ref):
-    across, _, width = sums_ref.shape
-    columns = (width - LANES) // 2
+    across, count, columns = out_ref.shape
     total = sums_ref[0].astype(jnp.float32)
     for i in range(1, across):
         total = total + sums_ref[i].astype(jnp.float32)
-    squares = total[:, 2 * columns : 2 * columns + 1] + total[:, 2 * columns + 1 : 2 * columns + 2]
+    squares = total[:count, columns : columns + 1] + total[:count, columns + 1 : columns + 2]
     scale = lax.rsqrt(squares / full_width + EPSILON)
-    gate = total[:, :columns] * scale
-    lift = total[:, columns : 2 * columns] * scale
+    gate = total[:count, :columns] * scale
+    lift = total[count:, :columns] * scale
     hidden = (gate / (1.0 + jnp.exp(-gate)) * lift).astype(jnp.bfloat16)
     for i in range(across):
         out_ref[i] = hidden
@@ -213,7 +213,7 @@
     whole = pl.BlockSpec(memory_space=pltpu.VMEM)
     return pl.pallas_call(
         functools.partial(hidden_kernel, full_width),
-        out_shape=pltpu.VMEM((across, count, (width - LANES) // 2), jnp.bfloat16),
+        out_shape=pltpu.VMEM((across, count // 2, width - LANES), jnp.bfloat16),
         in_specs=[whole],
         out_specs=whole,
         compiler_params=pltpu.CompilerParams(vmem_limit_bytes=8 << 20),

time: 211 us -> 213 us (level)
  no operation moved by 1% of the time
where the time goes in v1:
time: 213 us; the launch traced here: 212 us
  blocking collectives  119 us (56%)
  starting transfers between devices  52 us (24%)
  waiting for transfers between devices  33.1 us (16%)
  Pallas kernels  5.45 us (3%)
    all_to_all x2, blocking collectives, between_segments(): lax.all_to_all(blocks, EXPERT, split_axis=0, concat_axis=0, tiled=True, a...  82.4 us
    ppermute x14, starting transfers between devices, from_partner(): lax.ppermute(x, axis, [(i, i ^ apart) for i in range(lax.axis_size(axis))])  52 us
    ppermute x14, waiting for transfers between devices, from_partner(): lax.ppermute(x, axis, [(i, i ^ apart) for i in range(lax.axis_size(axis))])  33.1 us
    all_to_all x1, blocking collectives, through_expert(): lax.all_to_all(sums, 'tensor', split_axis=0, concat_axis=0, tiled=True)  24.3 us
    all_to_all x1, blocking collectives, through_expert(): lax.all_to_all(copies, 'tensor', split_axis=0, concat_axis=0, tiled=True)  12.2 us
  transfers between devices with their start and end apart: 14, of which 8 were waited for; matrix products, arithmetic and copies ran while one was open for 0% of the time, Pallas kernels for 0%

profile of v1, /device:TPU:40, one launch (start us, length us, event | category | flops | bytes accessed | tf_op | source)
XLA Modules:
  0.0 211.9 jit_solution(17438867470779692530)
XLA Ops:
  0.0 1.9 pack.1
  1.9 0.2 reshape.29
  2.0 0.0 copy-start.1
  2.0 0.0 copy-start.2
  2.0 0.0 copy-start.3
  2.1 61.9 %all_to_all.20 = bf16[4,108,128]{2,1,0:T(8,128)(2,1)S(1)} all-to-all(bf16[4,108,128]{2,1,0:T(8,128)(2,1)S(1)} %reshape.29), channel_id=1, replica_groups={{0,64,160,224},{4,68,164,228},{8,72,168,232},{12,76,172,236},{16,80,176..., dimensions={0} | all-to-all | bytes 221184 | tf_op jit(solution)/shard_map/all_to_all | solution.py:145
  64.0 0.2 reshape.30
  64.1 13.4 %collective-permute-start = (bf16[36,1536]{1,0:T(8,128)(2,1)S(1)}, bf16[36,1536]{1,0:T(8,128)(2,1)S(1)}, u32[]{:S(2)}, u32[]{:S(2)}) collective-permute-start(bf16[36,1536]{1,0:T(8,128)(2,1)S(1)} %reshape.30), channel_id=1, source_target_pairs={{0,32},{8,40},{16,48},{24,56},{32,0},{40,8},{48,16},{56,24},{1,33}... | collective-permute-start | bytes 331784 | tf_op jit(solution)/shard_map/ppermute | solution.py:23
  77.5 2.3 %collective-permute-start.1 = (bf16[36,1536]{1,0:T(8,128)(2,1)S(1)}, bf16[36,1536]{1,0:T(8,128)(2,1)S(1)}, u32[]{:S(2)}, u32[]{:S(2)}) collective-permute-start(bf16[36,1536]{1,0:T(8,128)(2,1)S(1)} %reshape.30), channel_id=1, source_target_pairs={{0,16},{8,24},{16,0},{24,8},{32,48},{40,56},{48,32},{56,40},{1,17}... | collective-permute-start | bytes 331784 | tf_op jit(solution)/shard_map/ppermute | solution.py:23
  79.8 5.3 %collective-permute-done = bf16[36,1536]{1,0:T(8,128)(2,1)S(1)} collective-permute-done((bf16[36,1536]{1,0:T(8,128)(2,1)S(1)}, bf16[36,1536]{1,0:T(8,128)(2,1)S(1)}, u32[]{:S(2)}, u32[]{:S(2)}) %collective-permute-start) | collective-permute-done | bytes 110624 | tf_op jit(solution)/shard_map/ppermute | solution.py:23
  85.1 4.2 %collective-permute-start.2 = (bf16[36,1536]{1,0:T(8,128)(2,1)S(1)}, bf16[36,1536]{1,0:T(8,128)(2,1)S(1)}, u32[]{:S(2)}, u32[]{:S(2)}) collective-permute-start(bf16[36,1536]{1,0:T(8,128)(2,1)S(1)} %collective-permute-done), channel_id=1, source_target_pairs={{0,16},{8,24},{16,0},{24,8},{32,48},{40,56},{48,32},{56,40},{1,17}... | collective-permute-start | bytes 331784 | tf_op jit(solution)/shard_map/ppermute | solution.py:23
  89.4 2.7 %collective-permute-start.3 = (bf16[72,1536]{1,0:T(8,128)(2,1)S(1)}, bf16[72,1536]{1,0:T(8,128)(2,1)S(1)}, u32[]{:S(2)}, u32[]{:S(2)}) collective-permute-start(bf16[72,1536]{1,0:T(8,128)(2,1)S(1)} %pad_maximum_fusion.1), channel_id=1, source_target_pairs={{0,8},{8,0},{16,24},{24,16},{32,40},{40,32},{48,56},{56,48},{1,9},... | collective-permute-start | bytes 663560 | tf_op jit(solution)/shard_map/ppermute | solution.py:23
  92.1 0.0 collective-permute-done.1
  92.1 2.3 %collective-permute-done.2 = bf16[36,1536]{1,0:T(8,128)(2,1)S(1)} collective-permute-done((bf16[36,1536]{1,0:T(8,128)(2,1)S(1)}, bf16[36,1536]{1,0:T(8,128)(2,1)S(1)}, u32[]{:S(2)}, u32[]{:S(2)}) %collective-permute-start.2) | collective-permute-done | bytes 110624 | tf_op jit(solution)/shard_map/ppermute | solution.py:23
  94.5 2.4 %collective-permute-start.4 = (bf16[72,1536]{1,0:T(8,128)(2,1)S(1)}, bf16[72,1536]{1,0:T(8,128)(2,1)S(1)}, u32[]{:S(2)}, u32[]{:S(2)}) collective-permute-start(bf16[72,1536]{1,0:T(8,128)(2,1)S(1)} %pad_maximum_fusion.2), channel_id=1, source_target_pairs={{0,8},{8,0},{16,24},{24,16},{32,40},{40,32},{48,56},{56,48},{1,9},... | collective-permute-start | bytes 663560 | tf_op jit(solution)/shard_map/ppermute | solution.py:23
  96.9 0.1 pad_maximum_fusion.refs_0_
  97.0 2.0 collective-permute-start.5
  99.0 0.6 collective-permute-done.3
  99.6 3.7 %collective-permute-done.4 = bf16[72,1536]{1,0:T(8,128)(2,1)S(1)} collective-permute-done((bf16[72,1536]{1,0:T(8,128)(2,1)S(1)}, bf16[72,1536]{1,0:T(8,128)(2,1)S(1)}, u32[]{:S(2)}, u32[]{:S(2)}) %collective-permute-start.4) | collective-permute-done | bytes 221216 | tf_op jit(solution)/shard_map/ppermute | solution.py:23
  103.4 2.0 collective-permute-start.6
  105.3 0.0 collective-permute-done.5.refs_2_
  105.4 1.7 collective-permute-done.6.refs_3_
  107.1 0.0 copy-done.1
  107.1 0.0 copy-done.2
  107.1 0.0 copy-done.3
  107.1 2.2 %up.1 = bf16[4,288,640]{2,1,0:T(8,128)(2,1)S(1)} custom-call(bf16[144,1536]{1,0:T(8,128)(2,1)S(1)} %pad_maximum_fusion.refs_0_, bf16[144,1536]{1,0:T(8,128)(2,1)S(1)} %constant_dynamic-update-slice_fusion.refs_1_, bf16[144,1536]{1,0:T(8,128)(2,1)S(1)} %collective-permute-done.5.refs_2_, bf16[144,1536]{1,0:T(8,128)(2,1)S(1)} %collective-permute-done.6.refs_3_, ...), custom_call_target="tpu_custom_call" | custom-call | tf_op jit(solution)/shard_map/up/pallas_call | solution.py:186
  109.3 24.3 %all_to_all.21.sums_ref = bf16[4,288,640]{2,1,0:T(8,128)(2,1)S(1)} all-to-all(bf16[4,288,640]{2,1,0:T(8,128)(2,1)S(1)} %up.1), channel_id=1, replica_groups=mesh['parts'=2,'seg'=4,'pos'=8,'core'=2,'tensor'=4] {'tensor'}, dimensions={0} | all-to-all | bytes 2949120 | tf_op jit(solution)/shard_map/all_to_all | solution.py:287
  133.7 0.0 copy-start
  133.7 0.3 hidden.1
  134.0 12.2 %all_to_all.22.hidden_ref = bf16[4,144,512]{2,1,0:T(8,128)(2,1)S(1)} all-to-all(bf16[4,144,512]{2,1,0:T(8,128)(2,1)S(1)} %hidden.1), channel_id=1, replica_groups=mesh['parts'=2,'seg'=4,'pos'=8,'core'=2,'tensor'=4] {'tensor'}, dimensions={0} | all-to-all | bytes 1179648 | tf_op jit(solution)/shard_map/all_to_all | solution.py:289
  146.1 0.0 copy-done
  146.1 1.1 down.1
  147.2 2.0 collective-permute-start.8
  149.2 2.4 %collective-permute-start.7 = (bf16[144,1536]{1,0:T(8,128)(2,1)S(1)}, bf16[144,1536]{1,0:T(8,128)(2,1)S(1)}, u32[]{:S(2)}, u32[]{:S(2)}) collective-permute-start(bf16[144,1536]{1,0:T(8,128)(2,1)S(1)} %get-tuple-element.18), channel_id=1, source_target_pairs={{0,4},{4,0},{1,5},{5,1},{2,6},{6,2},{3,7},{7,3},{8,12},{12,8},{9,1... | collective-permute-start | bytes 1327112 | tf_op jit(solution)/shard_map/ppermute | solution.py:23
  151.6 0.0 collective-permute-done.8
  151.6 0.1 add_convert_fusion
  151.8 2.7 %collective-permute-start.10 = (bf16[72,1536]{1,0:T(8,128)(2,1)S(1)}, bf16[72,1536]{1,0:T(8,128)(2,1)S(1)}, u32[]{:S(2)}, u32[]{:S(2)}) collective-permute-start(bf16[72,1536]{1,0:T(8,128)(2,1)S(1)} %get-tuple-element.25), channel_id=1, source_target_pairs={{0,8},{8,0},{16,24},{24,16},{32,40},{40,32},{48,56},{56,48},{1,9},... | collective-permute-start | bytes 663560 | tf_op jit(solution)/shard_map/ppermute | solution.py:23
  154.4 0.0 collective-permute-done.7
  154.5 0.1 convert_add_fusion
  154.6 0.1 fusion.4
  154.6 3.2 %collective-permute-start.9 = (bf16[72,1536]{1,0:T(8,128)(2,1)S(1)}, bf16[72,1536]{1,0:T(8,128)(2,1)S(1)}, u32[]{:S(2)}, u32[]{:S(2)}) collective-permute-start(bf16[72,1536]{1,0:T(8,128)(2,1)S(1)} %get-tuple-element.26), channel_id=1, source_target_pairs={{0,8},{8,0},{16,24},{24,16},{32,40},{40,32},{48,56},{56,48},{1,9},... | collective-permute-start | bytes 663560 | tf_op jit(solution)/shard_map/ppermute | solution.py:23
  157.9 4.1 %collective-permute-done.10 = bf16[72,1536]{1,0:T(8,128)(2,1)S(1)} collective-permute-done((bf16[72,1536]{1,0:T(8,128)(2,1)S(1)}, bf16[72,1536]{1,0:T(8,128)(2,1)S(1)}, u32[]{:S(2)}, u32[]{:S(2)}) %collective-permute-start.10) | collective-permute-done | bytes 221216 | tf_op jit(solution)/shard_map/ppermute | solution.py:23
  162.1 4.3 %collective-permute-start.12 = (bf16[36,1536]{1,0:T(8,128)(2,1)S(1)}, bf16[36,1536]{1,0:T(8,128)(2,1)S(1)}, u32[]{:S(2)}, u32[]{:S(2)}) collective-permute-start(bf16[36,1536]{1,0:T(8,128)(2,1)S(1)} %get-tuple-element.28), channel_id=1, source_target_pairs={{0,16},{8,24},{16,0},{24,8},{32,48},{40,56},{48,32},{56,40},{1,17}... | collective-permute-start | bytes 331784 | tf_op jit(solution)/shard_map/ppermute | solution.py:23
  166.4 2.5 %collective-permute-start.11 = (bf16[36,1536]{1,0:T(8,128)(2,1)S(1)}, bf16[36,1536]{1,0:T(8,128)(2,1)S(1)}, u32[]{:S(2)}, u32[]{:S(2)}) collective-permute-start(bf16[36,1536]{1,0:T(8,128)(2,1)S(1)} %get-tuple-element.27), channel_id=1, source_target_pairs={{0,16},{8,24},{16,0},{24,8},{32,48},{40,56},{48,32},{56,40},{1,17}... | collective-permute-start | bytes 331784 | tf_op jit(solution)/shard_map/ppermute | solution.py:23
  168.9 0.0 collective-permute-done.9
  168.9 0.1 convert_add_fusion.1
  169.0 4.9 %collective-permute-done.12 = bf16[36,1536]{1,0:T(8,128)(2,1)S(1)} collective-permute-done((bf16[36,1536]{1,0:T(8,128)(2,1)S(1)}, bf16[36,1536]{1,0:T(8,128)(2,1)S(1)}, u32[]{:S(2)}, u32[]{:S(2)}) %collective-permute-start.12) | collective-permute-done | bytes 110624 | tf_op jit(solution)/shard_map/ppermute | solution.py:23
  173.9 6.0 %collective-permute-start.13 = (bf16[36,1536]{1,0:T(8,128)(2,1)S(1)}, bf16[36,1536]{1,0:T(8,128)(2,1)S(1)}, u32[]{:S(2)}, u32[]{:S(2)}) collective-permute-start(bf16[36,1536]{1,0:T(8,128)(2,1)S(1)} %fusion.1), channel_id=1, source_target_pairs={{0,32},{8,40},{16,48},{24,56},{32,0},{40,8},{48,16},{56,24},{1,33}... | collective-permute-start | bytes 331784 | tf_op jit(solution)/shard_map/ppermute | solution.py:23
  179.9 0.0 collective-permute-done.11
  179.9 10.3 %collective-permute-done.13 = bf16[36,1536]{1,0:T(8,128)(2,1)S(1)} collective-permute-done((bf16[36,1536]{1,0:T(8,128)(2,1)S(1)}, bf16[36,1536]{1,0:T(8,128)(2,1)S(1)}, u32[]{:S(2)}, u32[]{:S(2)}) %collective-permute-start.13) | collective-permute-done | bytes 110624 | tf_op jit(solution)/shard_map/ppermute | solution.py:23
  190.3 0.2 reshape.31
  190.4 20.5 %all_to_all.23 = bf16[4,108,128]{2,1,0:T(8,128)(2,1)S(1)} all-to-all(bf16[4,108,128]{2,1,0:T(8,128)(2,1)S(1)} %reshape.31), channel_id=1, replica_groups={{0,64,160,224},{4,68,164,228},{8,72,168,232},{12,76,172,236},{16,80,176..., dimensions={0} | all-to-all | bytes 221184 | tf_op jit(solution)/shard_map/all_to_all | solution.py:145
  211.0 0.2 reshape.32
  211.1 0.8 fusion
  (9 shorter events, 0.3 us)
Async XLA Ops:
  2.0 105.1 %copy-start.1 = (bf16[1536,512]{1,0:T(8,128)(2,1)S(1)}, bf16[1536,512]{1,0:T(8,128)(2,1)}, u32[]{:S(2)}) copy-start(bf16[1536,512]{1,0:T(8,128)(2,1)} %refs_5_.3) | copy-start | bytes 4718596
  2.0 105.1 %copy-start.2 = (bf16[1536,512]{1,0:T(8,128)(2,1)S(1)}, bf16[1536,512]{1,0:T(8,128)(2,1)}, u32[]{:S(2)}) copy-start(bf16[1536,512]{1,0:T(8,128)(2,1)} %refs_6_.1) | copy-start | bytes 4718596
  2.0 105.1 %copy-start.3 = (f32[1536]{0:T(1024)S(1)}, f32[1536]{0:T(1024)}, u32[]{:S(2)}) copy-start(f32[1536]{0:T(1024)} %param.16) | copy-start | bytes 18436
  64.1 21.0 %collective-permute-start = (bf16[36,1536]{1,0:T(8,128)(2,1)S(1)}, bf16[36,1536]{1,0:T(8,128)(2,1)S(1)}, u32[]{:S(2)}, u32[]{:S(2)}) collective-permute-start(bf16[36,1536]{1,0:T(8,128)(2,1)S(1)} %reshape.30), channel_id=1, source_target_pairs={{0,32},{8,40},{16,48},{24,56},{32,0},{40,8},{48,16},{56,24},{1,33}... | collective-permute-start | bytes 331784 | tf_op jit(solution)/shard_map/ppermute | solution.py:23
  77.5 14.6 %collective-permute-start.1 = (bf16[36,1536]{1,0:T(8,128)(2,1)S(1)}, bf16[36,1536]{1,0:T(8,128)(2,1)S(1)}, u32[]{:S(2)}, u32[]{:S(2)}) collective-permute-start(bf16[36,1536]{1,0:T(8,128)(2,1)S(1)} %reshape.30), channel_id=1, source_target_pairs={{0,16},{8,24},{16,0},{24,8},{32,48},{40,56},{48,32},{56,40},{1,17}... | collective-permute-start | bytes 331784 | tf_op jit(solution)/shard_map/ppermute | solution.py:23
  85.1 9.4 %collective-permute-start.2 = (bf16[36,1536]{1,0:T(8,128)(2,1)S(1)}, bf16[36,1536]{1,0:T(8,128)(2,1)S(1)}, u32[]{:S(2)}, u32[]{:S(2)}) collective-permute-start(bf16[36,1536]{1,0:T(8,128)(2,1)S(1)} %collective-permute-done), channel_id=1, source_target_pairs={{0,16},{8,24},{16,0},{24,8},{32,48},{40,56},{48,32},{56,40},{1,17}... | collective-permute-start | bytes 331784 | tf_op jit(solution)/shard_map/ppermute | solution.py:23
  89.4 10.2 %collective-permute-start.3 = (bf16[72,1536]{1,0:T(8,128)(2,1)S(1)}, bf16[72,1536]{1,0:T(8,128)(2,1)S(1)}, u32[]{:S(2)}, u32[]{:S(2)}) collective-permute-start(bf16[72,1536]{1,0:T(8,128)(2,1)S(1)} %pad_maximum_fusion.1), channel_id=1, source_target_pairs={{0,8},{8,0},{16,24},{24,16},{32,40},{40,32},{48,56},{56,48},{1,9},... | collective-permute-start | bytes 663560 | tf_op jit(solution)/shard_map/ppermute | solution.py:23
  94.5 8.8 %collective-permute-start.4 = (bf16[72,1536]{1,0:T(8,128)(2,1)S(1)}, bf16[72,1536]{1,0:T(8,128)(2,1)S(1)}, u32[]{:S(2)}, u32[]{:S(2)}) collective-permute-start(bf16[72,1536]{1,0:T(8,128)(2,1)S(1)} %pad_maximum_fusion.2), channel_id=1, source_target_pairs={{0,8},{8,0},{16,24},{24,16},{32,40},{40,32},{48,56},{56,48},{1,9},... | collective-permute-start | bytes 663560 | tf_op jit(solution)/shard_map/ppermute | solution.py:23
  97.0 8.3 %collective-permute-start.5 = (bf16[144,1536]{1,0:T(8,128)(2,1)S(1)}, bf16[144,1536]{1,0:T(8,128)(2,1)S(1)}, u32[]{:S(2)}, u32[]{:S(2)}) collective-permute-start(bf16[144,1536]{1,0:T(8,128)(2,1)S(1)} %pad_maximum_fusion.refs_0_), channel_id=1, source_target_pairs={{0,4},{4,0},{1,5},{5,1},{2,6},{6,2},{3,7},{7,3},{8,12},{12,8},{9,1... | collective-permute-start | bytes 1327112 | tf_op jit(solution)/shard_map/ppermute | solution.py:23
  103.4 3.7 %collective-permute-start.6 = (bf16[144,1536]{1,0:T(8,128)(2,1)S(1)}, bf16[144,1536]{1,0:T(8,128)(2,1)S(1)}, u32[]{:S(2)}, u32[]{:S(2)}) collective-permute-start(bf16[144,1536]{1,0:T(8,128)(2,1)S(1)} %constant_dynamic-update-slice_fusion.refs_1_), channel_id=1, source_target_pairs={{0,4},{4,0},{1,5},{5,1},{2,6},{6,2},{3,7},{7,3},{8,12},{12,8},{9,1... | collective-permute-start | bytes 1327112 | tf_op jit(solution)/shard_map/ppermute | solution.py:23
  133.7 12.5 %copy-start = (bf16[512,1536]{1,0:T(8,128)(2,1)S(1)}, bf16[512,1536]{1,0:T(8,128)(2,1)}, u32[]{:S(2)}) copy-start(bf16[512,1536]{1,0:T(8,128)(2,1)} %weight_ref.1) | copy-start | bytes 4718596
  147.2 4.4 %collective-permute-start.8 = (bf16[144,1536]{1,0:T(8,128)(2,1)S(1)}, bf16[144,1536]{1,0:T(8,128)(2,1)S(1)}, u32[]{:S(2)}, u32[]{:S(2)}) collective-permute-start(bf16[144,1536]{1,0:T(8,128)(2,1)S(1)} %get-tuple-element.21), channel_id=1, source_target_pairs={{0,4},{4,0},{1,5},{5,1},{2,6},{6,2},{3,7},{7,3},{8,12},{12,8},{9,1... | collective-permute-start | bytes 1327112 | tf_op jit(solution)/shard_map/ppermute | solution.py:23
  149.2 5.3 %collective-permute-start.7 = (bf16[144,1536]{1,0:T(8,128)(2,1)S(1)}, bf16[144,1536]{1,0:T(8,128)(2,1)S(1)}, u32[]{:S(2)}, u32[]{:S(2)}) collective-permute-start(bf16[144,1536]{1,0:T(8,128)(2,1)S(1)} %get-tuple-element.18), channel_id=1, source_target_pairs={{0,4},{4,0},{1,5},{5,1},{2,6},{6,2},{3,7},{7,3},{8,12},{12,8},{9,1... | collective-permute-start | bytes 1327112 | tf_op jit(solution)/shard_map/ppermute | solution.py:23
  151.8 10.2 %collective-permute-start.10 = (bf16[72,1536]{1,0:T(8,128)(2,1)S(1)}, bf16[72,1536]{1,0:T(8,128)(2,1)S(1)}, u32[]{:S(2)}, u32[]{:S(2)}) collective-permute-start(bf16[72,1536]{1,0:T(8,128)(2,1)S(1)} %get-tuple-element.25), channel_id=1, source_target_pairs={{0,8},{8,0},{16,24},{24,16},{32,40},{40,32},{48,56},{56,48},{1,9},... | collective-permute-start | bytes 663560 | tf_op jit(solution)/shard_map/ppermute | solution.py:23
  154.6 14.3 %collective-permute-start.9 = (bf16[72,1536]{1,0:T(8,128)(2,1)S(1)}, bf16[72,1536]{1,0:T(8,128)(2,1)S(1)}, u32[]{:S(2)}, u32[]{:S(2)}) collective-permute-start(bf16[72,1536]{1,0:T(8,128)(2,1)S(1)} %get-tuple-element.26), channel_id=1, source_target_pairs={{0,8},{8,0},{16,24},{24,16},{32,40},{40,32},{48,56},{56,48},{1,9},... | collective-permute-start | bytes 663560 | tf_op jit(solution)/shard_map/ppermute | solution.py:23
  162.1 11.8 %collective-permute-start.12 = (bf16[36,1536]{1,0:T(8,128)(2,1)S(1)}, bf16[36,1536]{1,0:T(8,128)(2,1)S(1)}, u32[]{:S(2)}, u32[]{:S(2)}) collective-permute-start(bf16[36,1536]{1,0:T(8,128)(2,1)S(1)} %get-tuple-element.28), channel_id=1, source_target_pairs={{0,16},{8,24},{16,0},{24,8},{32,48},{40,56},{48,32},{56,40},{1,17}... | collective-permute-start | bytes 331784 | tf_op jit(solution)/shard_map/ppermute | solution.py:23
  166.4 13.5 %collective-permute-start.11 = (bf16[36,1536]{1,0:T(8,128)(2,1)S(1)}, bf16[36,1536]{1,0:T(8,128)(2,1)S(1)}, u32[]{:S(2)}, u32[]{:S(2)}) collective-permute-start(bf16[36,1536]{1,0:T(8,128)(2,1)S(1)} %get-tuple-element.27), channel_id=1, source_target_pairs={{0,16},{8,24},{16,0},{24,8},{32,48},{40,56},{48,32},{56,40},{1,17}... | collective-permute-start | bytes 331784 | tf_op jit(solution)/shard_map/ppermute | solution.py:23
  173.9 16.3 %collective-permute-start.13 = (bf16[36,1536]{1,0:T(8,128)(2,1)S(1)}, bf16[36,1536]{1,0:T(8,128)(2,1)S(1)}, u32[]{:S(2)}, u32[]{:S(2)}) collective-permute-start(bf16[36,1536]{1,0:T(8,128)(2,1)S(1)} %fusion.1), channel_id=1, source_target_pairs={{0,32},{8,40},{16,48},{24,56},{32,0},{40,8},{48,16},{56,24},{1,33}... | collective-permute-start | bytes 331784 | tf_op jit(solution)/shard_map/ppermute | solution.py:23
